TPU v7x, 32 devices: a whole 2x2x4 slice. The times are simulated.
32 devices in a mesh: code: 4 (over y, core), tok: 8 (over z, x).
Axes of the slice: x: 2, y: 2, z: 4, core: 2. Of those that a mesh axis runs over, the one named last changes fastest.
Arguments:
- tokens: bfloat16 [4096, 256], P('tok'), may hold values from -6 to 6
- codebook: bfloat16 [65536, 256], P('code'), may hold values from -2 to 2
- cotangent: bfloat16 [4096, 256], P('tok'), may hold values from -96 to 96
Outputs:
- quantized: float32 [4096, 256], P('tok', 'code')
- code_grad: float32 [65536, 256], P(('code', 'tok'))
All inputs are finite; a program needn't handle non-finite values.
Results may differ from a plain program's by a relative error of at most 0.006.
Values may be sent and summed in bfloat16 or wider, within the bound.
A program may use at most 128 MiB of HBM per device.

v0:
```python
import math

import jax
import jax.numpy as jnp
from jax import lax
from jax.sharding import PartitionSpec as P


def token_terms(book_rows, feats, grads, row_max, total, inner, scale):
    count = feats.shape[0]
    block = math.gcd(count, 2048)
    turns = count // block

    def step(index, acc):
        feat_block = lax.dynamic_slice_in_dim(feats, index * block, block, 0)
        grad_block = lax.dynamic_slice_in_dim(grads, index * block, block, 0)
        peak = lax.dynamic_slice_in_dim(row_max, index * block, block, 0)
        norm = lax.dynamic_slice_in_dim(total, index * block, block, 0)
        dotted = lax.dynamic_slice_in_dim(inner, index * block, block, 0)
        logits = scale * jnp.einsum(
            "td,kd->tk", feat_block, book_rows, preferred_element_type=jnp.float32
        )
        scores = jnp.einsum("td,kd->tk", grad_block, book_rows, preferred_element_type=jnp.float32)
        prob = jnp.exp(logits - peak[:, None]) / norm[:, None]
        dlogits = prob * (scores - dotted[:, None])
        first = jnp.einsum(
            "tk,td->kd", prob.astype(jnp.bfloat16), grad_block, preferred_element_type=jnp.float32
        )
        second = jnp.einsum(
            "tk,td->kd",
            dlogits.astype(jnp.bfloat16),
            feat_block,
            preferred_element_type=jnp.float32,
        )
        return acc + first + scale * second

    empty = jnp.zeros((book_rows.shape[0], book_rows.shape[1]), jnp.float32)
    return lax.fori_loop(0, turns, step, empty)


def per_device(tokens, codebook, cotangent):
    rows = tokens.shape[0]
    width = tokens.shape[1]
    codes_here = codebook.shape[0]
    scale = 2.0 / math.sqrt(width)
    block = min(512, rows)
    blocks = rows // block

    def local_pass(index):
        logits = scale * jnp.einsum(
            "td,kd->tk", tokens, codebook, preferred_element_type=jnp.float32
        )
        scores = jnp.einsum("td,kd->tk", cotangent, codebook, preferred_element_type=jnp.float32)
        local_max = jnp.max(logits, axis=1)
        weights = jnp.exp(logits - local_max[:, None]).astype(jnp.bfloat16)
        local_sum = jnp.sum(weights, axis=1, dtype=jnp.float32)
        local_dot = jnp.sum(weights * scores, axis=1, dtype=jnp.float32)
        local_vec = jnp.dot(weights, codebook, preferred_element_type=jnp.float32)
        return (local_max, local_sum, local_vec, local_dot)

    local_max, local_sum, local_vec, local_dot = lax.map(local_pass, jnp.arange(blocks))
    local_max = local_max.reshape(rows)
    local_sum = local_sum.reshape(rows)
    local_dot = local_dot.reshape(rows)
    local_vec = local_vec.reshape(rows, width)
    columns = width // lax.axis_size("code")
    offset = lax.axis_index("code") * columns
    row_max = lax.pmax(local_max, "code")
    factor = jnp.exp(local_max - row_max)
    total, dot_sum, vec_sum = lax.psum(
        (local_sum * factor, local_dot * factor, local_vec * factor[:, None]), "code"
    )
    share = lax.dynamic_slice_in_dim(vec_sum, offset, columns, 1)
    inner = dot_sum / total
    quantized = share / total[:, None]
    group_rows = codes_here // lax.axis_size("tok")
    mine = lax.dynamic_slice_in_dim(codebook, lax.axis_index("tok") * group_rows, group_rows, 0)
    every_max, every_total, every_inner = (
        lax.all_gather(row_max, "tok", axis=0, tiled=True),
        lax.all_gather(total, "tok", axis=0, tiled=True),
        lax.all_gather(inner, "tok", axis=0, tiled=True),
    )
    code_grad = token_terms(
        mine,
        lax.all_gather(tokens, "tok", axis=0, tiled=True),
        lax.all_gather(cotangent, "tok", axis=0, tiled=True),
        every_max,
        every_total,
        every_inner,
        scale,
    )
    return (quantized, code_grad)


def solution(mesh):
    return jax.shard_map(
        per_device,
        mesh=mesh,
        in_specs=(P("tok", None), P("code", None), P("tok", None)),
        out_specs=(P("tok", "code"), P(("code", "tok"), None)),
        check_vma=False,
    )
```

profile of v0, /device:TPU:0, one launch (start us, length us, event | category | flops | bytes accessed | tf_op | source)
XLA Modules:
  0.0 254.4 jit_solution(9441784418069896157)
XLA Ops:
  8.0 0.0 all-reduce.3.cloned.1.call-start
  8.0 15.3 %multiply_reduce_fusion = (f32[512]{0:T(512)S(1)}, f32[512,16384]{1,0:T(8,128)}) fusion(bf16[512,256]{1,0:T(8,128)(2,1)} %param.5, bf16[16384,256]{1,0:T(8,128)(2,1)} %param.6), kind=kOutput, calls=%fused_computation.18 | convolution fusion | flops 4311744000 | bytes 42207232 | tf_op jit(solution)/shard_map/while/body/eval_jaxpr/td,kd->tk/dot_general | solution.py:50
  23.4 8.4 %pmax.7 = f32[512]{0:T(512)S(1)} all-reduce(f32[512]{0:T(512)S(1)} %get-tuple-element.215), channel_id=1, replica_groups=mesh['code'=4,'tok'=8] {'code'}, use_global_device_ids=true, to_apply=%region_1.2 | all-reduce | flops 512 | bytes 4096 | tf_op jit(solution)/shard_map/pmax | solution.py:68
  31.8 0.0 copy-start.1
  31.8 20.0 %convert_reduce_fusion = (f32[512]{0:T(512)S(1)}, bf16[512,16384]{1,0:T(8,128)(2,1)}) fusion(f32[512]{0:T(512)S(1)} %get-tuple-element.215, f32[512,16384]{1,0:T(8,128)} %get-tuple-element.216), kind=kLoop, calls=%fused_computation.15 | loop fusion | flops 41942528 | bytes 50335744 | tf_op jit(solution)/shard_map/while/body/eval_jaxpr/reduce_sum | solution.py:56
  51.7 0.0 copy-done.1
  51.8 10.7 %fusion.15 = f32[512]{0:T(512)S(1)} fusion(bf16[512,16384]{1,0:T(8,128)(2,1)} %get-tuple-element.214, bf16[512,256]{1,0:T(8,128)(2,1)S(1)} %copy-done.1, bf16[16384,256]{1,0:T(8,128)(2,1)} %param.6), kind=kOutput, calls=%fused_computation.16 | convolution fusion | flops 4320132608 | bytes 25430016 | tf_op jit(solution)/shard_map/while/body/eval_jaxpr/td,kd->tk/dot_general | solution.py:53
  62.5 13.2 %convolution_multiply_fusion.1 = f32[512,256]{0,1:T(8,128)} fusion(bf16[512,16384]{1,0:T(8,128)(2,1)} %get-tuple-element.214, bf16[16384,256]{1,0:T(8,128)(2,1)} %param.6, f32[512]{0:T(512)S(1)} %get-tuple-element.212), kind=kOutput, calls=%fused_computation.19 | convolution fusion | flops 4295098368 | bytes 25692160 | tf_op jit(solution)/shard_map/while/body/eval_jaxpr/dot_general | solution.py:58
  75.7 0.0 all-reduce.3.cloned.1.call-update
  75.7 0.0 all-gather.6.cloned.1.call-start
  75.8 0.5 all-gather.6.cloned.1.call-update
  76.3 0.0 all-gather.8.cloned.1.call-start
  76.3 0.5 all-gather.8.cloned.1.call-update
  76.9 5.8 %all-reduce = (f32[512]{0:T(512)S(1)}, f32[512]{0:T(512)S(1)}) all-reduce(f32[512]{0:T(512)S(1)} %mul.64, f32[512]{0:T(512)S(1)} %get-tuple-element.211), channel_id=1, replica_groups=mesh['code'=4,'tok'=8] {'code'}, use_global_device_ids=true, to_apply=%region_4.5 | all-reduce | flops 1024 | bytes 8192 | tf_op jit(solution)/shard_map/psum | solution.py:70
  82.7 26.8 %all-gather.2 = f32[8,1,512]{2,1,0:T(1,128)S(1)} all-gather(f32[1,1,512]{2,1,0:T(1,128)S(1)} %bitcast.23), channel_id=1, replica_groups=mesh['code'=4,'tok'=8] {'tok'}, dimensions={0}, use_global_device_ids=true | all-gather | bytes 18432 | tf_op jit(solution)/shard_map/all_gather | solution.py:81
  109.4 26.5 %all-gather.1 = f32[8,1,512]{2,1,0:T(1,128)S(1)} all-gather(f32[1,1,512]{2,1,0:T(1,128)S(1)} %bitcast.21), channel_id=1, replica_groups=mesh['code'=4,'tok'=8] {'tok'}, dimensions={0}, use_global_device_ids=true | all-gather | bytes 18432 | tf_op jit(solution)/shard_map/all_gather | solution.py:80
  136.0 26.4 %all-gather = f32[8,1,512]{2,1,0:T(1,128)S(1)} all-gather(f32[1,1,512]{2,1,0:T(1,128)S(1)} %bitcast.22), channel_id=1, replica_groups=mesh['code'=4,'tok'=8] {'tok'}, dimensions={0}, use_global_device_ids=true | all-gather | bytes 18432 | tf_op jit(solution)/shard_map/all_gather | solution.py:79
  162.4 1.3 constant_dynamic-slice_fusion
  163.7 0.0 all-reduce.3.cloned.1.call-done
  163.7 1.6 dynamic-slice_divide_fusion
  165.3 0.0 all-gather.6.cloned.1.call-done
  165.3 12.3 %all-gather.8.cloned.1.call-done = bf16[4096,256]{1,0:T(8,128)(2,1)} async-done(((bf16[512,256]{1,0:T(8,128)(2,1)}), bf16[4096,256]{1,0:T(8,128)(2,1)}) %all-gather.8.cloned.1.call-update) | async-done | bytes 2097168 | tf_op jit(solution)/shard_map/all_gather | solution.py:86
  177.5 68.1 %while.9 = (s32[]{:T(128)}, f32[2048,256]{1,0:T(8,128)S(1)}, bf16[4096,256]{1,0:T(8,128)(2,1)}, bf16[2048,256]{1,0:T(8,128)(2,1)S(1)}, f32[4096]{0:T(1024)S(1)},...) while((s32[]{:T(128)}, f32[2048,256]{1,0:T(8,128)S(1)}, ...), condition=%wide.region_8.9_spmd.clone, body=%wide.region_7.8_spmd.clone.sunk | while | flops 8621391872 | bytes 65086656 | solution.py:38
  177.5 8.5 %exponential_divide_fusion.2 = f32[2048,2048]{1,0:T(8,128)} fusion(bf16[2048,256]{1,0:T(8,128)(2,1)S(1)} %get-tuple-element.293, f32[2048]{0:T(1024)S(1)} %dynamic_slice.70, f32[2048]{0:T(1024)S(1)} %dynamic_slice.71, bf16[4096,256]{1,0:T(8,128)(2,1)} %get-tuple-element.292, s32[]{:T(128)S(6)} %select_n.21), kind=kOutput, calls=%fused_computation.1.clone.1 | convolution fusion | flops 2160066560 | bytes 18890756 | tf_op jit(solution)/shard_map/while/body/eval_jaxpr/td,kd->tk/dot_general | solution.py:20
  186.1 9.8 %fusion.41 = f32[2048,256]{1,0:T(8,128)} fusion(f32[2048,2048]{1,0:T(8,128)} %exponential_divide_fusion.2, f32[2048,256]{1,0:T(8,128)S(1)} %get-tuple-element.279, pred[]{:T(512)S(6)} %compare.3, bf16[4096,256]{1,0:T(8,128)(2,1)} %get-tuple-element.296, s32[]{:T(128)S(6)} %select_n.21), kind=kOutput, calls=%fused_computation.6.clone.1 | convolution fusion | flops 2152726528 | bytes 22020100 | tf_op jit(solution)/shard_map/while/body/eval_jaxpr/tk,td->kd/dot_general | solution.py:26
  195.9 15.6 %fusion.42 = f32[2048,256]{1,0:T(8,128)S(1)} fusion(f32[2048,256]{1,0:T(8,128)} %fusion.41, f32[2048,2048]{1,0:T(8,128)} %exponential_divide_fusion.2, bf16[2048,256]{1,0:T(8,128)(2,1)S(1)} %get-tuple-element.293, f32[2048]{0:T(1024)S(1)} %dynamic_slice.72, bf16[4096,256]{1,0:T(8,128)(2,1)} %get-tuple-element.296, s32[]{:T(128)S(6)} %select_n.21, ...), kind=kOutput, calls=%fused_computation.5.clone.1 | convolution fusion | flops 4308598784 | bytes 24126464 | tf_op jit(solution)/shard_map/while/body/eval_jaxpr/tk,td->kd/dot_general | solution.py:29
  211.6 8.6 %exponential_divide_fusion.2 = f32[2048,2048]{1,0:T(8,128)} fusion(bf16[2048,256]{1,0:T(8,128)(2,1)S(1)} %get-tuple-element.293, f32[2048]{0:T(1024)S(1)} %dynamic_slice.70, f32[2048]{0:T(1024)S(1)} %dynamic_slice.71, bf16[4096,256]{1,0:T(8,128)(2,1)} %get-tuple-element.292, s32[]{:T(128)S(6)} %select_n.21), kind=kOutput, calls=%fused_computation.1.clone.1 | convolution fusion | flops 2160066560 | bytes 18890756 | tf_op jit(solution)/shard_map/while/body/eval_jaxpr/td,kd->tk/dot_general | solution.py:20
  220.2 9.8 %fusion.41 = f32[2048,256]{1,0:T(8,128)} fusion(f32[2048,2048]{1,0:T(8,128)} %exponential_divide_fusion.2, f32[2048,256]{1,0:T(8,128)S(1)} %get-tuple-element.279, pred[]{:T(512)S(6)} %compare.3, bf16[4096,256]{1,0:T(8,128)(2,1)} %get-tuple-element.296, s32[]{:T(128)S(6)} %select_n.21), kind=kOutput, calls=%fused_computation.6.clone.1 | convolution fusion | flops 2152726528 | bytes 22020100 | tf_op jit(solution)/shard_map/while/body/eval_jaxpr/tk,td->kd/dot_general | solution.py:26
  230.0 15.6 %fusion.42 = f32[2048,256]{1,0:T(8,128)S(1)} fusion(f32[2048,256]{1,0:T(8,128)} %fusion.41, f32[2048,2048]{1,0:T(8,128)} %exponential_divide_fusion.2, bf16[2048,256]{1,0:T(8,128)(2,1)S(1)} %get-tuple-element.293, f32[2048]{0:T(1024)S(1)} %dynamic_slice.72, bf16[4096,256]{1,0:T(8,128)(2,1)} %get-tuple-element.296, s32[]{:T(128)S(6)} %select_n.21, ...), kind=kOutput, calls=%fused_computation.5.clone.1 | convolution fusion | flops 4308598784 | bytes 24126464 | tf_op jit(solution)/shard_map/while/body/eval_jaxpr/tk,td->kd/dot_general | solution.py:29
  245.7 0.0 copy-start
  245.7 1.3 copy-done
  (10 shorter events, 0.0 us)
Async XLA Ops:
  8.0 155.7 %all-reduce.3.cloned.1.call-start = ((), (), s32[]{:S(2)}) async-start(), calls=%async_computation | async-start | bytes 1048576 | tf_op jit(solution)/shard_map/psum | solution.py:70
  31.8 20.0 %copy-start.1 = (bf16[512,256]{1,0:T(8,128)(2,1)S(1)}, bf16[512,256]{1,0:T(8,128)(2,1)}, u32[]{:S(2)}) copy-start(bf16[512,256]{1,0:T(8,128)(2,1)} %param.7) | copy-start | bytes 786436
  75.7 89.6 %all-gather.6.cloned.1.call-start = ((), (), s32[]{:S(2)}) async-start(), calls=%async_computation.1 | async-start | bytes 2359296 | tf_op jit(solution)/shard_map/all_gather | solution.py:85
  76.3 101.3 %all-gather.8.cloned.1.call-start = ((), (), s32[]{:S(2)}) async-start(), calls=%async_computation.2 | async-start | bytes 2359296 | tf_op jit(solution)/shard_map/all_gather | solution.py:86
  245.7 1.3 copy-start
Sparse Core Ops, SparseCore 0:
  75.8 33.7 all-reduce.2
Sparse Core Ops, SparseCore 1:
  78.3 49.3 all-gather.5
  129.7 47.8 all-gather.7
where the time goes:
time: 255 us; the launch traced here: 254 us
  matrix products  107 us (42%)
  blocking collectives  93.8 us (37%)
  other arithmetic  21.6 us (8%)
  between operations  15.5 us (6%)
  waiting for transfers between devices  13.4 us (5%)
  local copies, waits for them, and re-layouts  2.64 us (1%)
    dot_general x2, matrix products, step(): jnp.einsum('tk,td->kd', dlogits.astype(jnp.bfloat16), feat_block, preferr...  31.3 us
    all_gather x1, blocking collectives, per_device(): lax.all_gather(inner, 'tok', axis=0, tiled=True)  26.8 us
    all_gather x1, blocking collectives, per_device(): lax.all_gather(total, 'tok', axis=0, tiled=True)  26.5 us
    all_gather x1, blocking collectives, per_device(): lax.all_gather(row_max, 'tok', axis=0, tiled=True)  26.4 us
    reduce_sum x1, other arithmetic, local_pass(): local_sum = jnp.sum(weights, axis=1, dtype=jnp.float32)  20 us
    dot_general x2, matrix products, step(): jnp.einsum('tk,td->kd', prob.astype(jnp.bfloat16), grad_block, preferred_...  19.7 us
    dot_general x2, matrix products, step(): jnp.einsum('td,kd->tk', feat_block, book_rows, preferred_element_type=jnp...  17.1 us
    dot_general x1, matrix products, local_pass(): jnp.einsum('td,kd->tk', tokens, codebook, preferred_element_type=jnp.floa...  15.3 us
  transfers between devices with their start and end apart: 3, of which 1 were waited for; matrix products, arithmetic and copies ran while one was open for 1% of the time, Pallas kernels for 0%

commit v1 on v0

v1 whole, which is shorter than its diff:
```python
import functools
import math

import jax
import jax.numpy as jnp
from jax import lax
from jax.experimental import pallas as pl
from jax.experimental.pallas import tpu as pltpu
from jax.sharding import PartitionSpec as P

LOG2E = 1.4426950408889634
NT = (((1,), (1,)), ((), ()))
RELAY_AFTER = {3: 1, 5: 2, 6: 3, 8: 4}
HANDOVER_AFTER = {5: 1, 7: 2, 8: 3}


def kernel(n_code, n_tok, tile, height, scale, tok_ref, cot_ref, book_hbm, quant_out, grad_out,
           book, slab, peak, total, vec, all_tok, all_cot, stat, final, q_send, q_recv,
           book_sem, own_sem, send1, recv1, send2, recv2, send3, recv3, s_send, s_recv, f_send, f_recv,
           qs_sem, qr_sem):
    mine_code = lax.axis_index("code")
    mine_tok = lax.axis_index("tok")
    rows, width = tok_ref.shape
    codes = book_hbm.shape[0]
    count = codes // tile
    parts = book_sem.shape[0]
    chunk = codes // parts
    per = chunk // tile
    rate = scale * LOG2E
    piece = rows // n_code
    columns = width // n_code

    book_copies = [
        pltpu.make_async_copy(
            book_hbm.at[pl.ds(i * chunk, chunk)], book.at[pl.ds(i * chunk, chunk)], book_sem.at[i]
        )
        for i in range(parts)
    ]
    for c in book_copies:
        c.start()

    barrier = pltpu.get_barrier_semaphore()
    for d in range(1, n_tok):
        pl.semaphore_signal(
            barrier, inc=1, device_id=(mine_code, lax.rem(mine_tok + d, n_tok)),
            device_id_type=pl.DeviceIdType.MESH,
        )
    for c in range(1, n_code):
        pl.semaphore_signal(
            barrier, inc=1, device_id=(lax.rem(mine_code + c, n_code), mine_tok),
            device_id_type=pl.DeviceIdType.MESH,
        )
    pl.semaphore_wait(barrier, n_tok - 1 + n_code - 1)

    def remote(src, dst, send, recv, code, tok):
        return pltpu.make_async_remote_copy(
            src_ref=src, dst_ref=dst, send_sem=send, recv_sem=recv,
            device_id=(code, tok), device_id_type=pl.DeviceIdType.MESH,
        )

    def first_copies(d):
        at = pl.ds(pl.multiple_of(mine_code * piece, piece), piece)
        to = lax.rem(mine_tok + d, n_tok)
        return [
            remote(ref.at[at], every.at[mine_tok, at], send1.at[d - 1, j], recv1.at[d - 1, j], mine_code, to)
            for j, (ref, every) in enumerate(((tok_ref, all_tok), (cot_ref, all_cot)))
        ]

    n_far = n_code // 2
    partner = mine_code + 1 - 2 * lax.rem(mine_code, 2)

    def pass_on(d, k, send, recv, to):
        owner = lax.rem(mine_code - 2 * k + n_code, n_code)
        at = pl.ds(pl.multiple_of(owner * piece, piece), piece)
        block = lax.rem(mine_tok - d + n_tok, n_tok)
        return [
            remote(every.at[block, at], every.at[block, at], send.at[j], recv.at[j], to, mine_tok)
            for j, every in enumerate((all_tok, all_cot))
        ]

    def far_copies(d, k):
        to = lax.rem(mine_code + 2 * k, n_code)
        return pass_on(d, 0, send2.at[d - 1, k - 1], recv2.at[d - 1, k - 1], to)

    def near_copies(d, k):
        return pass_on(d, k, send3.at[d - 1, k], recv3.at[d - 1, k], partner)

    for d in range(1, n_tok):
        for copy in first_copies(d):
            copy.start()
    own = [
        pltpu.make_async_copy(tok_ref, all_tok.at[mine_tok], own_sem.at[0]),
        pltpu.make_async_copy(cot_ref, all_cot.at[mine_tok], own_sem.at[1]),
    ]
    for copy in own:
        copy.start()

    def relay(d):
        for copy in first_copies(d):
            copy.wait_recv()
        for k in range(1, n_far):
            for copy in far_copies(d, k):
                copy.start()
        for copy in near_copies(d, 0):
            copy.start()

    def hand_over(d):
        for k in range(1, n_far):
            for copy in far_copies(d, k):
                copy.wait_recv()
            for copy in near_copies(d, k):
                copy.start()

    def produce(index, slot):
        part_rows = book[pl.ds(pl.multiple_of(index * tile, tile), tile), :]
        logits = lax.dot_general(tok_ref[...], part_rows, NT, preferred_element_type=jnp.float32)
        slab[slot] = logits
        top = logits[:, 0:128]
        for j in range(1, tile // 128):
            top = jnp.maximum(top, logits[:, j * 128:(j + 1) * 128])
        return jnp.broadcast_to(jnp.max(top, axis=1, keepdims=True) * rate, top.shape)

    def consume(index, slot, new):
        old = peak[...]
        fresh = jnp.maximum(old, new)
        peak[...] = fresh
        alpha = jnp.exp2(old - fresh)
        part = total[...] * alpha
        pieces = []
        for j in range(tile // 128):
            w = jnp.exp2(slab[slot, :, j * 128:(j + 1) * 128] * rate - fresh)
            part = part + w
            pieces.append(w.astype(jnp.bfloat16))
        total[...] = part
        weights = jnp.concatenate(pieces, axis=1)
        part_rows = book[pl.ds(pl.multiple_of(index * tile, tile), tile), :]
        update = jnp.dot(weights, part_rows, preferred_element_type=jnp.float32)
        vec[...] = vec[...] * jnp.concatenate([alpha] * (width // 128), axis=1) + update

    peak[...] = jnp.full_like(peak, -1e30)
    total[...] = jnp.zeros_like(total)
    vec[...] = jnp.zeros_like(vec)
    grad_out[...] = jnp.zeros_like(grad_out)
    book_copies[0].wait()
    top = produce(0, 0)
    relayed = handed = 0
    for part in range(parts):
        first = part * per
        last = part + 1 == parts
        if not last:
            book_copies[part + 1].wait()

        def pair(step, top):
            index = first + 2 * step
            nxt = produce(index + 1, 1)
            consume(index, 0, top)
            after = produce(index + 2, 0)
            consume(index + 1, 1, nxt)
            return after

        turns = per // 2 - (1 if last else 0)
        if turns == 1:
            top = pair(0, top)
        elif turns > 1:
            top = lax.fori_loop(0, turns, pair, top)
        if last:
            nxt = produce(count - 1, 1)
            consume(count - 2, 0, top)
            consume(count - 1, 1, nxt)
        d = RELAY_AFTER.get(part + 1)
        if d is not None and d < n_tok:
            relay(d)
            relayed = d
        d = HANDOVER_AFTER.get(part + 1)
        if d is not None and d < n_tok:
            hand_over(d)
            handed = d

    dot = jnp.sum(vec[...] * cot_ref[...].astype(jnp.float32), axis=1, keepdims=True)
    summed = jnp.sum(total[...], axis=1, keepdims=True)
    lane = lax.broadcasted_iota(jnp.int32, (rows, 128), 1)
    packed = jnp.where(lane == 0, peak[...], jnp.where(lane == 1, summed, dot))
    stat[mine_code] = jnp.transpose(packed)[0:8, :]

    def stat_copy(c):
        return remote(stat.at[mine_code], stat.at[mine_code], s_send.at[c - 1], s_recv.at[c - 1],
                      lax.rem(mine_code + c, n_code), mine_tok)

    for c in range(1, n_code):
        stat_copy(c).start()
    for c in range(1, n_code):
        stat_copy(c).wait_recv()
    row_max = stat[0, 0:1, :]
    for c in range(1, n_code):
        row_max = jnp.maximum(row_max, stat[c, 0:1, :])
    norm = jnp.zeros_like(row_max)
    dots = jnp.zeros_like(row_max)
    for c in range(n_code):
        factor = jnp.exp2(stat[c, 0:1, :] - row_max)
        norm = norm + factor * stat[c, 1:2, :]
        dots = dots + factor * stat[c, 2:3, :]
    shift = row_max + jnp.log(norm) * LOG2E
    inner = dots / norm
    row = lax.broadcasted_iota(jnp.int32, (8, rows), 0)
    final[mine_tok] = jnp.where(row == 0, shift, inner)

    def final_copy(d):
        return remote(final.at[mine_tok], final.at[mine_tok], f_send.at[d - 1], f_recv.at[d - 1],
                      mine_code, lax.rem(mine_tok + d, n_tok))

    for d in range(1, n_tok):
        final_copy(d).start()

    gain = jnp.exp2(stat[mine_code, 0:1, :] - shift)
    turned = jnp.transpose(vec[...]) * gain
    for c in range(n_code):
        q_send[c] = turned[c * columns:(c + 1) * columns, :]

    def quant_copy(c):
        to = lax.rem(mine_code + c, n_code)
        return remote(q_send.at[to], q_recv.at[c - 1], qs_sem.at[c - 1], qr_sem.at[c - 1], to, mine_tok)

    for copy in own:
        copy.wait()

    group = grad_out.shape[0]
    base = mine_tok * group

    def block_step(step, carry):
        @pl.when(step + relayed + 1 < n_tok)
        def _():
            relay(step + relayed + 1)

        @pl.when(step + handed + 1 < n_tok)
        def _():
            hand_over(step + handed + 1)

        @pl.when(step == n_tok // 2)
        def _():
            for c in range(1, n_code):
                quant_copy(c).start()

        @pl.when(step > 0)
        def _():
            final_copy(step).wait_recv()
            for k in range(n_far):
                for copy in near_copies(step, k):
                    copy.wait_recv()

        block = lax.rem(mine_tok - step + n_tok, n_tok)
        tok = all_tok[block]
        cot = all_cot[block]
        move = final[block, 0:1, :]
        middle = final[block, 1:2, :]
        other = jnp.concatenate([cot, (tok.astype(jnp.float32) * scale).astype(jnp.bfloat16)], axis=0)

        def half(h, carry):
            at = pl.ds(pl.multiple_of(h * height, height), height)
            codes_at = book[pl.ds(pl.multiple_of(base + h * height, height), height), :]
            logits = lax.dot_general(codes_at, tok, NT, preferred_element_type=jnp.float32)
            scores = lax.dot_general(codes_at, cot, NT, preferred_element_type=jnp.float32)
            prob = jnp.exp2(logits * rate - move)
            dlog = prob * (scores - middle)
            both = jnp.concatenate([prob.astype(jnp.bfloat16), dlog.astype(jnp.bfloat16)], axis=1)
            grad_out[at, :] += jnp.dot(both, other, preferred_element_type=jnp.float32)
            return carry

        return lax.fori_loop(0, group // height, half, carry)

    lax.fori_loop(0, n_tok, block_step, 0)

    result = q_send[mine_code]
    for c in range(1, n_code):
        quant_copy(c).wait_recv()
        result = result + q_recv[c - 1]
    quant_out[...] = result
    for c in range(1, n_code):
        quant_copy(c).wait_send()
        stat_copy(c).wait_send()

    def drain(d, carry):
        for copy in first_copies(d):
            copy.wait_send()
        final_copy(d).wait_send()
        for k in range(n_far):
            for copy in near_copies(d, k):
                copy.wait_send()
            if k:
                for copy in far_copies(d, k):
                    copy.wait_send()
        return carry

    lax.fori_loop(1, n_tok, drain, 0)


def per_device(tokens, codebook, cotangent):
    rows, width = tokens.shape
    codes = codebook.shape[0]
    n_code, n_tok = lax.axis_size("code"), lax.axis_size("tok")
    scale = 2.0 / math.sqrt(width)
    group = codes // n_tok
    tile = min(1024, codes // 2)
    parts = min(8, codes // (2 * tile))
    columns = width // n_code
    dma = pltpu.SemaphoreType.DMA
    vmem = pl.BlockSpec(memory_space=pltpu.VMEM)
    turned, grad = pl.pallas_call(
        functools.partial(kernel, n_code, n_tok, tile, min(1024, group), scale),
        out_shape=(
            jax.ShapeDtypeStruct((columns, rows), jnp.float32),
            jax.ShapeDtypeStruct((group, width), jnp.float32),
        ),
        in_specs=[vmem, vmem, pl.BlockSpec(memory_space=pl.ANY)],
        out_specs=(vmem, vmem),
        scratch_shapes=[
            pltpu.VMEM((codes, width), jnp.bfloat16),
            pltpu.VMEM((2, rows, tile), jnp.float32),
            pltpu.VMEM((rows, 128), jnp.float32),
            pltpu.VMEM((rows, 128), jnp.float32),
            pltpu.VMEM((rows, width), jnp.float32),
            pltpu.VMEM((n_tok, rows, width), jnp.bfloat16),
            pltpu.VMEM((n_tok, rows, width), jnp.bfloat16),
            pltpu.VMEM((n_code, 8, rows), jnp.float32),
            pltpu.VMEM((n_tok, 8, rows), jnp.float32),
            pltpu.VMEM((n_code, columns, rows), jnp.float32),
            pltpu.VMEM((n_code - 1, columns, rows), jnp.float32),
            dma((parts,)),
            dma((2,)),
            dma((n_tok - 1, 2)),
            dma((n_tok - 1, 2)),
            dma((n_tok - 1, n_code // 2 - 1, 2)),
            dma((n_tok - 1, n_code // 2 - 1, 2)),
            dma((n_tok - 1, n_code // 2, 2)),
            dma((n_tok - 1, n_code // 2, 2)),
            dma((n_code - 1,)),
            dma((n_code - 1,)),
            dma((n_tok - 1,)),
            dma((n_tok - 1,)),
            dma((n_code - 1,)),
            dma((n_code - 1,)),
        ],
        compiler_params=pltpu.CompilerParams(
            collective_id=0, has_side_effects=True, vmem_limit_bytes=60 * 1024 * 1024
        ),
        cost_estimate=pl.CostEstimate(
            flops=12 * rows * codes * width, bytes_accessed=codes * width * 2,
            transcendentals=2 * rows * codes,
        ),
        name="quantize",
    )(tokens, cotangent, codebook)
    return turned.T, grad


def solution(mesh):
    return jax.shard_map(
        per_device,
        mesh=mesh,
        in_specs=(P("tok", None), P("code", None), P("tok", None)),
        out_specs=(P("tok", "code"), P(("code", "tok"), None)),
        check_vma=False,
    )
```

time: 255 us -> 69.6 us (0.27)
  matrix products: 107 us -> 0 us
  blocking collectives: 93.8 us -> 0 us
  Pallas kernels: 0 us -> 64.1 us
  other arithmetic: 21.6 us -> 0 us
  between operations: 15.5 us -> 0.64 us
  waiting for transfers between devices: 13.4 us -> 0 us
    dot_general x9 -> x0, matrix products: 107 us -> none  [the longest x2 31.3 us: step(): jnp.einsum('tk,td->kd', dlogits.astype(jnp.bfloat16), feat_block, preferr...]
    all_gather x3 -> x0, blocking collectives: 79.7 us -> none  [the longest x1 26.8 us: per_device(): lax.all_gather(inner, 'tok', axis=0, tiled=True)]
    pallas_call x0 -> x1, Pallas kernels: none -> 64.1 us  [per_device(): pl.pallas_call(functools.partial(kernel, n_code, n_tok, tile, min(1024, g...]
    reduce_sum x1 -> x0, other arithmetic: 20 us -> none  [local_pass(): local_sum = jnp.sum(weights, axis=1, dtype=jnp.float32)]
    all_gather x2 -> x0, waiting for transfers between devices: 12.3 us -> none  [the longest x1 12.3 us: per_device(): lax.all_gather(cotangent, 'tok', axis=0, tiled=True)]
    pmax x1 -> x0, blocking collectives: 8.36 us -> none  [per_device(): row_max = lax.pmax(local_max, 'code')]
    psum x1 -> x0, blocking collectives: 5.76 us -> none  [per_device(): lax.psum((local_sum * factor, local_dot * factor, local_vec * factor[:, N...]
    unnamed x4 -> x2, local copies, waits for them, and re-layouts: 1.32 us -> 4.61 us
  transfers between devices with their start and end apart: 3 -> 0, of which waited for: 1 -> 0; matrix products, arithmetic and copies ran while one was open for 1% -> 0% of each run, Pallas kernels for 0% -> 0%
where the time goes in v1:
time: 69.6 us; the launch traced here: 69.4 us
  Pallas kernels  64.1 us (92%)
  local copies, waits for them, and re-layouts  4.61 us (7%)
    pallas_call x1, Pallas kernels, per_device(): pl.pallas_call(functools.partial(kernel, n_code, n_tok, tile, min(1024, g...  64.1 us
    unnamed x2, local copies, waits for them, and re-layouts  4.61 us

profile of v1, /device:TPU:0, one launch (start us, length us, event | category | flops | bytes accessed | tf_op | source)
XLA Modules:
  0.0 69.4 jit_solution(4388404424082086677)
XLA Ops:
  0.6 64.1 %quantize.1 = (f32[64,512]{1,0:T(8,128)}, f32[2048,256]{1,0:T(8,128)}) custom-call(bf16[512,256]{1,0:T(8,128)(2,1)} %tok_ref.1, bf16[512,256]{1,0:T(8,128)(2,1)} %cot_ref.1, bf16[16384,256]{1,0:T(8,128)(2,1)} %book_hbm.1), custom_call_target="tpu_custom_call" | custom-call | flops 25769803776 | bytes 8388608 | tf_op jit(solution)/shard_map/quantize/pallas_call | solution.py:307
  64.8 1.6 %copy.7 = f32[512,64]{0,1:T(8,128)} copy(f32[512,64]{0,1:T(8,128)} %bitcast.1) | data formatting | bytes 262144
  66.3 3.0 %copy.8 = f32[2048,256]{1,0:T(8,128)} copy(f32[2048,256]{1,0:T(8,128)} %get-tuple-element.9) | data formatting | bytes 4194304
